TPU v7x, 32 devices: a whole 2x2x4 slice. The times are simulated.
32 devices in a mesh: unit: 4 (over y, core), ep: 4 (over z), fsdp: 2 (over x).
Axes of the slice: x: 2, y: 2, z: 4, core: 2. Of those that a mesh axis runs over, the one named last changes fastest.
Arguments:
- w_down: float32 [256, 1024, 2048], P(('unit', 'ep'), None, 'fsdp'), parts along dimension 0, may hold values from -0.25 to 0.25
- router_weight: float32 [8192, 64], P(('unit', 'fsdp'), 'ep'), parts along dimension 0, may hold values from -0.125 to 0.125
- router_gain: float32 [8192], P(('unit', 'fsdp')), parts along dimension 0, may hold values from 0.25 to 1.75
Outputs:
- serve_down: bfloat16 [256, 1024, 2048], P(('unit', 'ep'), 'fsdp'), parts along dimension 0
- scale_down: float32 [256, 1024], P(('unit', 'ep'), 'fsdp'), parts along dimension 0
- serve_router: bfloat16 [8192, 64], P('unit'), parts along dimension 0
There are 4 independent parts, one for each index of `unit`. A program takes and returns all parts, laid end to end along the dimension named above; each array names one. Nothing has to cross between parts.
All inputs are finite; a program needn't handle non-finite values. Where the computation divides by a largest or mean magnitude, that divisor is 1e-20 or more.
Results may differ from a plain program's by a relative error of at most 0.001.
Values may be sent and summed in bfloat16 or wider, within the bound.
A program may use at most 256 MiB of HBM per device.

v0:
```python
import jax
import jax.numpy as jnp
from jax import lax
from jax.sharding import PartitionSpec as P

D_MODEL = 2048


def on_device(w_down, router_weight, router_gain):
    total_down = lax.psum(jnp.sum(jnp.abs(w_down), axis=2), "fsdp")
    scale_down = total_down / D_MODEL
    narrow_down = (w_down / jnp.expand_dims(scale_down, 2)).astype(jnp.bfloat16)
    serve_down = lax.all_to_all(narrow_down, "fsdp", split_axis=1, concat_axis=2, tiled=True)
    scale_down = lax.dynamic_slice_in_dim(
        scale_down, lax.axis_index("fsdp") * serve_down.shape[1], serve_down.shape[1], axis=1
    )
    part_router = (router_weight * router_gain[:, None]).astype(jnp.bfloat16)
    row_router = lax.all_gather(part_router, "fsdp", axis=0, tiled=True)
    serve_router = lax.all_gather(row_router, "ep", axis=1, tiled=True)
    return (serve_down, scale_down, serve_router)


def solution(mesh):
    return jax.shard_map(
        on_device,
        mesh=mesh,
        in_specs=(P(("unit", "ep"), None, "fsdp"), P(("unit", "fsdp"), "ep"), P(("unit", "fsdp"))),
        out_specs=(P(("unit", "ep"), "fsdp", None), P(("unit", "ep"), "fsdp"), P("unit", None)),
        check_vma=False,
    )
```

profile of v0, /device:TPU:0, one launch (start us, length us, event | category | flops | bytes accessed | tf_op | source)
XLA Modules:
  0.0 625.7 jit_solution(12388147618959563152)
XLA Ops:
  7.2 0.0 all-reduce.2.cloned.1.call-start
  7.2 21.4 %abs_reduce_fusion = f32[16,1024]{1,0:T(8,128)} fusion(f32[16,1024,1024]{2,1,0:T(8,128)} %param.3), kind=kLoop, calls=%fused_computation.2 | loop fusion | flops 33538048 | bytes 67174400 | tf_op jit(solution)/shard_map/reduce_sum | solution.py:10
  28.6 0.0 all-reduce.2.cloned.1.call-update
  28.7 23.8 %all-reduce.2.cloned.1.call-done = f32[16,1024]{1,0:T(8,128)} async-done(((f32[16,1024]{1,0:T(8,128)}), f32[16,1024]{1,0:T(8,128)}) %all-reduce.2.cloned.1.call-update) | async-done | bytes 65552 | tf_op jit(solution)/shard_map/psum | solution.py:10
  52.5 0.8 broadcast_multiply_fusion
  53.3 0.2 copy.7
  53.5 0.0 copy-start
  53.5 0.0 copy-start.1
  53.6 60.1 %fusion = bf16[16,1024,1024]{2,0,1:T(8,128)(2,1)} fusion(f32[16,1024,1024]{2,1,0:T(8,128)} %param.3, f32[16,1024]{0,1:T(8,128)S(1)} %copy.7), kind=kLoop, calls=%fused_computation.1 | loop fusion | flops 33554432 | bytes 100728832 | tf_op jit(solution)/shard_map/convert_element_type | solution.py:12
  113.7 13.0 %all-to-all-start = ((bf16[16,1024,1024]{2,0,1:T(8,128)(2,1)}), bf16[16,1024,1024]{2,0,1:T(8,128)(2,1)}, u32[]{:S(2)}, u32[]{:S(2)}) async-start(bf16[16,1024,1024]{2,0,1:T(8,128)(2,1)} %fusion), calls=%async_computation | async-start | bytes 67108864 | tf_op jit(solution)/shard_map/all_to_all | solution.py:13
  126.6 0.0 copy-done
  126.6 0.0 copy-done.1
  126.7 362.4 %all_gather.6 = bf16[2048,16]{0,1:T(8,128)(2,1)S(1)} all-gather(bf16[1024,16]{0,1:T(8,128)(2,1)S(1)} %multiply_convert_fusion), channel_id=1, replica_groups=mesh['unit'=4,'ep'=4,'fsdp'=2] {'fsdp'}, dimensions={0}, use_global_device_ids=true | all-gather | bytes 98304 | tf_op jit(solution)/shard_map/all_gather | solution.py:18
  489.0 13.8 %all_gather.7 = bf16[2048,64]{0,1:T(8,128)(2,1)S(1)} all-gather(bf16[2048,16]{0,1:T(8,128)(2,1)S(1)} %all_gather.6), channel_id=1, replica_groups=mesh['unit'=4,'ep'=4,'fsdp'=2] {'ep'}, dimensions={1}, use_global_device_ids=true | all-gather | bytes 327680 | tf_op jit(solution)/shard_map/all_gather | solution.py:19
  502.9 0.6 constant_dynamic-slice_fusion
  503.5 0.0 all-to-all-done
  503.5 60.5 %copy.9 = bf16[16,512,2,1024]{3,2,1,0:T(2,128)(2,1)} copy(bf16[16,512,2,1024]{3,0,1,2:T(8,128)(2,1)} %bitcast.1) | data formatting | bytes 67108864 | tf_op jit(solution)/shard_map/all_to_all | solution.py:13
  564.0 54.2 %all_to_all.16 = bf16[16,512,2048]{2,1,0:T(8,128)(2,1)} reshape(bf16[16,512,2,1024]{3,2,1,0:T(2,128)(2,1)} %copy.9) | data formatting | bytes 67108864 | tf_op jit(solution)/shard_map/all_to_all | solution.py:13
  618.2 0.7 copy.15
  (1 shorter events, 0.0 us)
Async XLA Ops:
  7.2 45.3 %all-reduce.2.cloned.1.call-start = ((), (), s32[]{:S(2)}) async-start(), calls=%async_computation.1 | async-start | bytes 131072 | tf_op jit(solution)/shard_map/psum | solution.py:10
  53.5 73.1 %copy-start = (f32[1024,16]{0,1:T(8,128)S(1)}, f32[1024,16]{0,1:T(8,128)}, u32[]{:S(2)}) copy-start(f32[1024,16]{0,1:T(8,128)} %param.4) | copy-start | bytes 196612
  53.5 73.1 %copy-start.1 = (f32[1024]{0:T(1024)S(1)}, f32[1024]{0:T(1024)}, u32[]{:S(2)}) copy-start(f32[1024]{0:T(1024)} %param.5) | copy-start | bytes 12292
  113.7 389.8 %all-to-all-start = ((bf16[16,1024,1024]{2,0,1:T(8,128)(2,1)}), bf16[16,1024,1024]{2,0,1:T(8,128)(2,1)}, u32[]{:S(2)}, u32[]{:S(2)}) async-start(bf16[16,1024,1024]{2,0,1:T(8,128)(2,1)} %fusion), calls=%async_computation | async-start | bytes 67108864 | tf_op jit(solution)/shard_map/all_to_all | solution.py:13
Sparse Core Ops, SparseCore 0:
  28.8 23.6 all-reduce.1
where the time goes:
time: 627 us; the launch traced here: 626 us
  blocking collectives  376 us (60%)
  local copies, waits for them, and re-layouts  116 us (19%)
  other arithmetic  82.4 us (13%)
  waiting for transfers between devices  23.9 us (4%)
  between operations  14.1 us (2%)
  starting transfers between devices  13 us (2%)
    all_gather x1, blocking collectives, on_device(): row_router = lax.all_gather(part_router, 'fsdp', axis=0, tiled=True)  362 us
    all_to_all x2, local copies, waits for them, and re-layouts, on_device(): lax.all_to_all(narrow_down, 'fsdp', split_axis=1, concat_axis=2, tiled=True)  115 us
    convert_element_type x1, other arithmetic, on_device(): narrow_down = (w_down / jnp.expand_dims(scale_down, 2)).astype(jnp.bfloat16)  60.1 us
    psum x1, waiting for transfers between devices, on_device(): total_down = lax.psum(jnp.sum(jnp.abs(w_down), axis=2), 'fsdp')  23.8 us
    reduce_sum x1, other arithmetic, on_device(): total_down = lax.psum(jnp.sum(jnp.abs(w_down), axis=2), 'fsdp')  21.4 us
    all_gather x1, blocking collectives, on_device(): serve_router = lax.all_gather(row_router, 'ep', axis=1, tiled=True)  13.8 us
    all_to_all x1, starting transfers between devices, on_device(): lax.all_to_all(narrow_down, 'fsdp', split_axis=1, concat_axis=2, tiled=True)  13 us
  transfers between devices with their start and end apart: 2, of which 1 were waited for; matrix products, arithmetic and copies ran while one was open for 0% of the time, Pallas kernels for 0%

commit v1 on v0

--- a/solution.py
+++ b/solution.py
@@ -10,7 +10,12 @@
     total_down = lax.psum(jnp.sum(jnp.abs(w_down), axis=2), "fsdp")
     scale_down = total_down / D_MODEL
     narrow_down = (w_down / jnp.expand_dims(scale_down, 2)).astype(jnp.bfloat16)
-    serve_down = lax.all_to_all(narrow_down, "fsdp", split_axis=1, concat_axis=2, tiled=True)
+    serve_down = jnp.concatenate(
+        lax.all_to_all(
+            jnp.stack(jnp.split(narrow_down, lax.axis_size("fsdp"), axis=1)), "fsdp", 0, 0
+        ),
+        axis=2,
+    )
     scale_down = lax.dynamic_slice_in_dim(
         scale_down, lax.axis_index("fsdp") * serve_down.shape[1], serve_down.shape[1], axis=1
     )

time: 627 us -> 553 us (0.88)
  local copies, waits for them, and re-layouts: 116 us -> 47.7 us
    all_to_all x2 -> x0, local copies, waits for them, and re-layouts: 115 us -> none  [on_device(): lax.all_to_all(narrow_down, 'fsdp', split_axis=1, concat_axis=2, tiled=True)]
    convert_element_type x1, other arithmetic: 60.1 us -> 32.9 us  [on_device(): narrow_down = (w_down / jnp.expand_dims(scale_down, 2)).astype(jnp.bfloat16)]
    reshape x0 -> x1, local copies, waits for them, and re-layouts: none -> 23.3 us  [on_device(): jnp.concatenate(lax.all_to_all(jnp.stack(jnp.split(narrow_down, lax.axis_...]
    another operation x0 -> x1, local copies, waits for them, and re-layouts: none -> 23.1 us  [on_device(): jnp.stack(jnp.split(narrow_down, lax.axis_size('fsdp'), axis=1))]
    another operation x0 -> x1, other arithmetic: none -> 23 us  [on_device(): jnp.stack(jnp.split(narrow_down, lax.axis_size('fsdp'), axis=1))]
where the time goes in v1:
time: 553 us
  blocking collectives  376 us (68%)
  other arithmetic  78.1 us (14%)
  local copies, waits for them, and re-layouts  47.7 us (9%)
  waiting for transfers between devices  23.9 us (4%)
  between operations  14.1 us (3%)
  starting transfers between devices  13.1 us (2%)
    all_gather x1, blocking collectives, on_device(): row_router = lax.all_gather(part_router, 'fsdp', axis=0, tiled=True)  362 us
    convert_element_type x1, other arithmetic, on_device(): narrow_down = (w_down / jnp.expand_dims(scale_down, 2)).astype(jnp.bfloat16)  32.9 us
    psum x1, waiting for transfers between devices, on_device(): total_down = lax.psum(jnp.sum(jnp.abs(w_down), axis=2), 'fsdp')  23.8 us
    reshape x1, local copies, waits for them, and re-layouts, on_device(): jnp.concatenate(lax.all_to_all(jnp.stack(jnp.split(narrow_down, lax.axis_...  23.3 us
    another operation x1, local copies, waits for them, and re-layouts, on_device(): jnp.stack(jnp.split(narrow_down, lax.axis_size('fsdp'), axis=1))  23.1 us
    another operation x1, other arithmetic, on_device(): jnp.stack(jnp.split(narrow_down, lax.axis_size('fsdp'), axis=1))  23 us
    reduce_sum x1, other arithmetic, on_device(): total_down = lax.psum(jnp.sum(jnp.abs(w_down), axis=2), 'fsdp')  21.4 us
    all_gather x1, blocking collectives, on_device(): serve_router = lax.all_gather(row_router, 'ep', axis=1, tiled=True)  13.8 us
  transfers between devices with their start and end apart: 2, of which 1 were waited for; matrix products, arithmetic and copies ran while one was open for 0% of the time, Pallas kernels for 0%

profile of v1, /device:TPU:0, one launch (start us, length us, event | category | flops | bytes accessed | tf_op | source)
XLA Modules:
  0.0 553.1 jit_solution(2984466817001409051)
XLA Ops:
  7.2 0.0 all-reduce.2.cloned.1.call-start
  7.2 21.4 %abs_reduce_fusion = f32[16,1024]{1,0:T(8,128)} fusion(f32[16,1024,1024]{2,1,0:T(8,128)} %param.3), kind=kLoop, calls=%fused_computation.1 | loop fusion | flops 33538048 | bytes 67174400 | tf_op jit(solution)/shard_map/reduce_sum | solution.py:10
  28.6 0.0 all-reduce.2.cloned.1.call-update
  28.7 23.8 %all-reduce.2.cloned.1.call-done = f32[16,1024]{1,0:T(8,128)} async-done(((f32[16,1024]{1,0:T(8,128)}), f32[16,1024]{1,0:T(8,128)}) %all-reduce.2.cloned.1.call-update) | async-done | bytes 65552 | tf_op jit(solution)/shard_map/psum | solution.py:10
  52.5 0.8 broadcast_multiply_fusion
  53.3 32.9 %divide_convert_fusion = bf16[16,1024,1024]{2,1,0:T(8,128)(2,1)} fusion(f32[16,1024,1024]{2,1,0:T(8,128)} %param.3, f32[16,1024]{1,0:T(8,128)S(1)} %broadcast_multiply_fusion), kind=kLoop, calls=%fused_computation | loop fusion | flops 33554432 | bytes 100728832 | tf_op jit(solution)/shard_map/convert_element_type | solution.py:12
  86.2 23.1 %slice_bitcast_fusion.1 = (bf16[1,16,512,1024]{3,2,1,0:T(8,128)(2,1)}, bf16[1,16,512,1024]{3,2,1,0:T(8,128)(2,1)}) fusion(bf16[16,1024,1024]{2,1,0:T(8,128)(2,1)} %divide_convert_fusion), kind=kLoop, calls=%fused_computation.4 | loop fusion | bytes 67108864 | tf_op jit(solution)/shard_map/stack | solution.py:15
  109.3 23.0 %pad_maximum_fusion = bf16[2,16,512,1024]{3,2,1,0:T(8,128)(2,1)} fusion(bf16[1,16,512,1024]{3,2,1,0:T(8,128)(2,1)} %get-tuple-element.4, bf16[1,16,512,1024]{3,2,1,0:T(8,128)(2,1)} %get-tuple-element.3), kind=kLoop, calls=%fused_computation.2 | loop fusion | flops 16777216 | bytes 67108864 | tf_op jit(solution)/shard_map/stack | solution.py:15
  132.3 0.0 copy-start
  132.3 0.0 copy-start.1
  132.3 13.1 %all-to-all-start = ((bf16[2,16,512,1024]{3,2,1,0:T(8,128)(2,1)}), bf16[2,16,512,1024]{3,2,1,0:T(8,128)(2,1)}, u32[]{:S(2)}, u32[]{:S(2)}) async-start(bf16[2,16,512,1024]{3,2,1,0:T(8,128)(2,1)} %pad_maximum_fusion), calls=%async_computation | async-start | bytes 67108864 | tf_op jit(solution)/shard_map/all_to_all | solution.py:14
  145.4 0.0 copy-done
  145.4 0.0 copy-done.1
  145.5 362.4 %all_gather.6 = bf16[2048,16]{0,1:T(8,128)(2,1)S(1)} all-gather(bf16[1024,16]{0,1:T(8,128)(2,1)S(1)} %multiply_convert_fusion), channel_id=1, replica_groups=mesh['unit'=4,'ep'=4,'fsdp'=2] {'fsdp'}, dimensions={0}, use_global_device_ids=true | all-gather | bytes 98304 | tf_op jit(solution)/shard_map/all_gather | solution.py:23
  507.8 13.8 %all_gather.7 = bf16[2048,64]{0,1:T(8,128)(2,1)S(1)} all-gather(bf16[2048,16]{0,1:T(8,128)(2,1)S(1)} %all_gather.6), channel_id=1, replica_groups=mesh['unit'=4,'ep'=4,'fsdp'=2] {'ep'}, dimensions={1}, use_global_device_ids=true | all-gather | bytes 327680 | tf_op jit(solution)/shard_map/all_gather | solution.py:24
  521.7 0.6 constant_dynamic-slice_fusion
  522.3 0.0 all-to-all-done
  522.3 23.3 %copy.7 = bf16[2,16,64,8,1024]{4,3,0,2,1:T(8,128)(2,1)} copy(bf16[2,16,64,8,1024]{4,3,2,1,0:T(8,128)(2,1)} %bitcast.3) | data formatting | bytes 67108864 | tf_op jit(solution)/shard_map/reshape | solution.py:13
  545.6 0.7 copy.10
  (1 shorter events, 0.0 us)
Async XLA Ops:
  7.2 45.3 %all-reduce.2.cloned.1.call-start = ((), (), s32[]{:S(2)}) async-start(), calls=%async_computation.1 | async-start | bytes 131072 | tf_op jit(solution)/shard_map/psum | solution.py:10
  132.3 13.1 %copy-start = (f32[1024,16]{0,1:T(8,128)S(1)}, f32[1024,16]{0,1:T(8,128)}, u32[]{:S(2)}) copy-start(f32[1024,16]{0,1:T(8,128)} %param.4) | copy-start | bytes 196612
  132.3 13.1 %copy-start.1 = (f32[1024]{0:T(1024)S(1)}, f32[1024]{0:T(1024)}, u32[]{:S(2)}) copy-start(f32[1024]{0:T(1024)} %param.5) | copy-start | bytes 12292
  132.3 390.0 %all-to-all-start = ((bf16[2,16,512,1024]{3,2,1,0:T(8,128)(2,1)}), bf16[2,16,512,1024]{3,2,1,0:T(8,128)(2,1)}, u32[]{:S(2)}, u32[]{:S(2)}) async-start(bf16[2,16,512,1024]{3,2,1,0:T(8,128)(2,1)} %pad_maximum_fusion), calls=%async_computation | async-start | bytes 67108864 | tf_op jit(solution)/shard_map/all_to_all | solution.py:14
Sparse Core Ops, SparseCore 0:
  28.8 23.6 all-reduce.1
